TPU v7x, 32 devices: a whole 2x2x4 slice. The times are simulated.
32 devices in a mesh: gene: 8 (over z, x), cell: 4 (over y, core).
Axes of the slice: x: 2, y: 2, z: 4, core: 2. Of those that a mesh axis runs over, the one named last changes fastest.
Arguments:
- pool_counts: bfloat16 [20480, 16384], P('gene', 'cell'), may hold values from 0 to 6.5
- cell_picks: int32 [7, 4096], P(None, 'cell'), may hold values from 0 to 16383, as said below
- loadings_init: float32 [64, 20480], P(None, 'gene'), may hold values from -0.0390625 to 0.0390625
Outputs:
- scaled_loadings: float32 [64, 20480], P(None, 'gene')
Inputs may be any that keep to these rules, and one draw needn't show every extreme that they name: `cell_picks`: column b of every row names a pool cell in [(b // 1024) * 4096, (b // 1024 + 1) * 4096); no cell is named twice in one row.
All inputs are finite; a program needn't handle non-finite values.
Results may differ from a plain program's by a relative error of at most 0.018.
Values may be sent and summed in bfloat16 or wider, within the bound.
A program may use at most 128 MiB of HBM per device.

v0:
```python
import math
import jax
import jax.numpy as jnp
from jax import lax
from jax.sharding import PartitionSpec as P

STEPS = 7
step_rate = 1.0


def transposed_product(left, right):
    return lax.dot_general(
        left, right, (((1,), (1,)), ((), ())), preferred_element_type=jnp.float32
    )


def shards(pool_counts, cell_picks, loadings_init):
    loadings = loadings_init
    local_pool = pool_counts.shape[1]
    group = lax.axis_index("cell")
    batch_total = cell_picks.shape[1] * lax.axis_size("cell")
    gene_total = loadings.shape[1] * lax.axis_size("gene")
    for step_index in range(STEPS):
        chosen = cell_picks[step_index] - group * local_pool
        gathered = jnp.take(pool_counts, chosen, axis=1)
        weights_low = loadings.astype(jnp.bfloat16)
        product = jnp.dot(weights_low, gathered, preferred_element_type=jnp.float32)
        local_sums = jnp.sum(gathered, axis=1, dtype=jnp.float32)
        batch_means = lax.psum(local_sums, "cell") / batch_total
        shift = jnp.dot(
            weights_low.astype(jnp.float32), batch_means, precision=lax.Precision.HIGHEST
        )
        partial_value = product - shift[:, None]
        scores = lax.psum(partial_value, "gene")
        scores_low = scores.astype(jnp.bfloat16)
        raw_update = transposed_product(scores_low, gathered)
        row_totals = jnp.sum(scores_low, axis=1, dtype=jnp.float32)
        local_update = (raw_update - row_totals[:, None] * batch_means[None, :]) / batch_total
        update = lax.psum(local_update.astype(jnp.bfloat16), "cell").astype(jnp.float32)
        stepped = loadings + step_rate * update
        gram_part = jnp.dot(stepped, stepped.T, precision=lax.Precision.HIGHEST)
        gram_matrix = lax.psum(gram_part, "gene")
        factor = jnp.linalg.cholesky(gram_matrix)
        loadings = lax.linalg.triangular_solve(factor, stepped, left_side=True, lower=True)
    return loadings * math.sqrt(gene_total)


def solution(mesh):
    placed = (P("gene", "cell"), P(None, "cell"), P(None, "gene"))
    return jax.shard_map(
        shards, mesh=mesh, in_specs=placed, out_specs=P(None, "gene"), check_vma=False
    )
```

profile of v0, /device:TPU:0, one launch (start us, length us, event | category | flops | bytes accessed | tf_op | source)
XLA Modules:
  0.0 1143.4 jit_solution(7488319310404820462)
XLA Ops:
  7.8 25.9 %copy.4 = bf16[2560,4096]{0,1:T(8,128)(2,1)} copy(bf16[2560,4096]{1,0:T(8,128)(2,1)} %param.8) | data formatting | bytes 41943040 | tf_op args[0]
  33.7 20.2 %gather_fusion.6 = bf16[1024,2560]{1,0:T(8,128)(2,1)} fusion(bf16[2560,4096]{0,1:T(8,128)(2,1)} %copy.4, s32[1024]{0:T(1024)S(1)} %fusion.188), kind=kCustom, calls=%fused_computation.6.clone | custom fusion | bytes 10489856 | tf_op jit(solution)/shard_map/jit(_take)/gather | solution.py:25
  53.8 20.1 %gather_fusion.5 = bf16[1024,2560]{1,0:T(8,128)(2,1)} fusion(bf16[2560,4096]{0,1:T(8,128)(2,1)} %copy.4, s32[1024]{0:T(1024)S(1)} %fusion.187), kind=kCustom, calls=%fused_computation.5.clone | custom fusion | bytes 10489856 | tf_op jit(solution)/shard_map/jit(_take)/gather | solution.py:25
  73.9 20.5 %gather_fusion.4 = bf16[1024,2560]{1,0:T(8,128)(2,1)} fusion(bf16[2560,4096]{0,1:T(8,128)(2,1)} %copy.4, s32[1024]{0:T(1024)S(1)} %fusion.186), kind=kCustom, calls=%fused_computation.4.clone | custom fusion | bytes 10489856 | tf_op jit(solution)/shard_map/jit(_take)/gather | solution.py:25
  94.5 20.1 %gather_fusion.3 = bf16[1024,2560]{1,0:T(8,128)(2,1)} fusion(bf16[2560,4096]{0,1:T(8,128)(2,1)} %copy.4, s32[1024]{0:T(1024)S(1)} %fusion.185), kind=kCustom, calls=%fused_computation.3.clone | custom fusion | bytes 10489856 | tf_op jit(solution)/shard_map/jit(_take)/gather | solution.py:25
  114.6 20.2 %gather_fusion.2 = bf16[1024,2560]{1,0:T(8,128)(2,1)} fusion(bf16[2560,4096]{0,1:T(8,128)(2,1)} %copy.4, s32[1024]{0:T(1024)S(1)} %fusion.184), kind=kCustom, calls=%fused_computation.2.clone | custom fusion | bytes 10489856 | tf_op jit(solution)/shard_map/jit(_take)/gather | solution.py:25
  134.8 20.1 %gather_fusion.1 = bf16[1024,2560]{1,0:T(8,128)(2,1)} fusion(bf16[2560,4096]{0,1:T(8,128)(2,1)} %copy.4, s32[1024]{0:T(1024)S(1)} %fusion.183), kind=kCustom, calls=%fused_computation.1.clone | custom fusion | bytes 10489856 | tf_op jit(solution)/shard_map/jit(_take)/gather | solution.py:25
  154.9 20.1 %gather_fusion = bf16[1024,2560]{1,0:T(8,128)(2,1)} fusion(bf16[2560,4096]{0,1:T(8,128)(2,1)} %copy.4, s32[1024]{0:T(1024)S(1)} %fusion.182), kind=kCustom, calls=%fused_computation.clone | custom fusion | bytes 10489856 | tf_op jit(solution)/shard_map/jit(_take)/gather | solution.py:25
  179.3 7.3 convert_reduce_fusion
  195.6 33.5 %all-reduce.31.cloned.1.call-done = (f32[2560]{0:T(1024)}, f32[2560]{0:T(1024)}, f32[2560]{0:T(1024)}, f32[2560]{0:T(1024)}, f32[2560]{0:T(1024)}, /*index=5*/f32[2560]{0:T(1024)}, f32[2560]{0:T(1024)}) async-done(((f32[2560]{0:T(1024)}, f32[2560]{0:T(1024)}, f32[2560]{0:T(1024)}, f32[2560]{0:T(1024)}, f32[2560]{0:T(1024)}, /*index=5*/f32[2560]{0:T(1024)}, f32[2560]{0:T(1024)}), (f32[2560]{0:T(1024)}, ...) | async-done | bytes 71696 | tf_op jit(solution)/shard_map/psum | solution.py:29
  234.5 40.8 %all-reduce.32 = bf16[64,1024]{1,0:T(8,128)(2,1)S(1)} all-reduce(f32[64,1024]{1,0:T(8,128)S(1)} %fusion.94), channel_id=1, replica_groups=mesh['gene'=8,'cell'=4] {'gene'}, use_global_device_ids=true, to_apply=%region_2.4 | all-reduce | flops 65536 | bytes 393216 | tf_op jit(solution)/shard_map/psum | solution.py:34
  279.9 30.0 %all-reduce.17.cloned.1.call-done = bf16[64,2560]{1,0:T(8,128)(2,1)} async-done(((bf16[64,2560]{1,0:T(8,128)(2,1)}), bf16[64,2560]{1,0:T(8,128)(2,1)}) %all-reduce.17.cloned.1.call-update) | async-done | bytes 327696 | tf_op jit(solution)/shard_map/psum | solution.py:39
  311.8 37.1 %psum.199 = f32[64,64]{0,1:T(8,128)S(1)} all-reduce(f32[64,64]{0,1:T(8,128)S(1)} %fusion.116), channel_id=1, replica_groups=mesh['gene'=8,'cell'=4] {'gene'}, use_global_device_ids=true, to_apply=%region_5.7 | all-reduce | flops 4096 | bytes 32768 | tf_op jit(solution)/shard_map/psum | solution.py:42
  367.4 36.0 %all-reduce.33 = bf16[64,1024]{1,0:T(8,128)(2,1)S(1)} all-reduce(f32[64,1024]{1,0:T(8,128)S(1)} %fusion.97), channel_id=1, replica_groups=mesh['gene'=8,'cell'=4] {'gene'}, use_global_device_ids=true, to_apply=%region_10.0 | all-reduce | flops 65536 | bytes 393216 | tf_op jit(solution)/shard_map/psum | solution.py:34
  408.1 30.5 %all-reduce.19.cloned.1.call-done = bf16[64,2560]{1,0:T(8,128)(2,1)} async-done(((bf16[64,2560]{1,0:T(8,128)(2,1)}), bf16[64,2560]{1,0:T(8,128)(2,1)}) %all-reduce.19.cloned.1.call-update) | async-done | bytes 327696 | tf_op jit(solution)/shard_map/psum | solution.py:39
  440.4 37.6 %psum.203 = f32[64,64]{0,1:T(8,128)S(1)} all-reduce(f32[64,64]{0,1:T(8,128)S(1)} %fusion.118), channel_id=1, replica_groups=mesh['gene'=8,'cell'=4] {'gene'}, use_global_device_ids=true, to_apply=%region_13.0 | all-reduce | flops 4096 | bytes 32768 | tf_op jit(solution)/shard_map/psum | solution.py:42
  496.6 36.0 %all-reduce.34 = bf16[64,1024]{1,0:T(8,128)(2,1)S(1)} all-reduce(f32[64,1024]{1,0:T(8,128)S(1)} %fusion.100), channel_id=1, replica_groups=mesh['gene'=8,'cell'=4] {'gene'}, use_global_device_ids=true, to_apply=%region_16.0 | all-reduce | flops 65536 | bytes 393216 | tf_op jit(solution)/shard_map/psum | solution.py:34
  537.2 30.6 %all-reduce.21.cloned.1.call-done = bf16[64,2560]{1,0:T(8,128)(2,1)} async-done(((bf16[64,2560]{1,0:T(8,128)(2,1)}), bf16[64,2560]{1,0:T(8,128)(2,1)}) %all-reduce.21.cloned.1.call-update) | async-done | bytes 327696 | tf_op jit(solution)/shard_map/psum | solution.py:39
  569.7 37.1 %psum.207 = f32[64,64]{0,1:T(8,128)S(1)} all-reduce(f32[64,64]{0,1:T(8,128)S(1)} %fusion.120), channel_id=1, replica_groups=mesh['gene'=8,'cell'=4] {'gene'}, use_global_device_ids=true, to_apply=%region_19.0 | all-reduce | flops 4096 | bytes 32768 | tf_op jit(solution)/shard_map/psum | solution.py:42
  625.3 36.0 %all-reduce.35 = bf16[64,1024]{1,0:T(8,128)(2,1)S(1)} all-reduce(f32[64,1024]{1,0:T(8,128)S(1)} %fusion.103), channel_id=1, replica_groups=mesh['gene'=8,'cell'=4] {'gene'}, use_global_device_ids=true, to_apply=%region_22.0 | all-reduce | flops 65536 | bytes 393216 | tf_op jit(solution)/shard_map/psum | solution.py:34
  666.2 30.4 %all-reduce.23.cloned.1.call-done = bf16[64,2560]{1,0:T(8,128)(2,1)} async-done(((bf16[64,2560]{1,0:T(8,128)(2,1)}), bf16[64,2560]{1,0:T(8,128)(2,1)}) %all-reduce.23.cloned.1.call-update) | async-done | bytes 327696 | tf_op jit(solution)/shard_map/psum | solution.py:39
  698.4 37.1 %psum.211 = f32[64,64]{0,1:T(8,128)S(1)} all-reduce(f32[64,64]{0,1:T(8,128)S(1)} %fusion.122), channel_id=1, replica_groups=mesh['gene'=8,'cell'=4] {'gene'}, use_global_device_ids=true, to_apply=%region_25.0 | all-reduce | flops 4096 | bytes 32768 | tf_op jit(solution)/shard_map/psum | solution.py:42
  735.6 5.8 cholesky.152
  754.0 36.0 %all-reduce.36 = bf16[64,1024]{1,0:T(8,128)(2,1)S(1)} all-reduce(f32[64,1024]{1,0:T(8,128)S(1)} %fusion.106), channel_id=1, replica_groups=mesh['gene'=8,'cell'=4] {'gene'}, use_global_device_ids=true, to_apply=%region_28.0 | all-reduce | flops 65536 | bytes 393216 | tf_op jit(solution)/shard_map/psum | solution.py:34
  794.6 30.7 %all-reduce.25.cloned.1.call-done = bf16[64,2560]{1,0:T(8,128)(2,1)} async-done(((bf16[64,2560]{1,0:T(8,128)(2,1)}), bf16[64,2560]{1,0:T(8,128)(2,1)}) %all-reduce.25.cloned.1.call-update) | async-done | bytes 327696 | tf_op jit(solution)/shard_map/psum | solution.py:39
  827.1 37.1 %psum.215 = f32[64,64]{0,1:T(8,128)S(1)} all-reduce(f32[64,64]{0,1:T(8,128)S(1)} %fusion.124), channel_id=1, replica_groups=mesh['gene'=8,'cell'=4] {'gene'}, use_global_device_ids=true, to_apply=%region_31.0 | all-reduce | flops 4096 | bytes 32768 | tf_op jit(solution)/shard_map/psum | solution.py:42
  882.8 36.2 %all-reduce.37 = bf16[64,1024]{1,0:T(8,128)(2,1)S(1)} all-reduce(f32[64,1024]{1,0:T(8,128)S(1)} %fusion.109), channel_id=1, replica_groups=mesh['gene'=8,'cell'=4] {'gene'}, use_global_device_ids=true, to_apply=%region_34.0 | all-reduce | flops 65536 | bytes 393216 | tf_op jit(solution)/shard_map/psum | solution.py:34
  923.6 30.5 %all-reduce.27.cloned.1.call-done = bf16[64,2560]{1,0:T(8,128)(2,1)} async-done(((bf16[64,2560]{1,0:T(8,128)(2,1)}), bf16[64,2560]{1,0:T(8,128)(2,1)}) %all-reduce.27.cloned.1.call-update) | async-done | bytes 327696 | tf_op jit(solution)/shard_map/psum | solution.py:39
  956.0 37.1 %psum.219 = f32[64,64]{0,1:T(8,128)S(1)} all-reduce(f32[64,64]{0,1:T(8,128)S(1)} %fusion.126), channel_id=1, replica_groups=mesh['gene'=8,'cell'=4] {'gene'}, use_global_device_ids=true, to_apply=%region_37.0 | all-reduce | flops 4096 | bytes 32768 | tf_op jit(solution)/shard_map/psum | solution.py:42
  1011.6 35.9 %all-reduce.38 = bf16[64,1024]{1,0:T(8,128)(2,1)S(1)} all-reduce(f32[64,1024]{1,0:T(8,128)S(1)} %fusion.112), channel_id=1, replica_groups=mesh['gene'=8,'cell'=4] {'gene'}, use_global_device_ids=true, to_apply=%region_40.0 | all-reduce | flops 65536 | bytes 393216 | tf_op jit(solution)/shard_map/psum | solution.py:34
  1052.1 30.7 %all-reduce.29.cloned.1.call-done = bf16[64,2560]{1,0:T(8,128)(2,1)} async-done(((bf16[64,2560]{1,0:T(8,128)(2,1)}), bf16[64,2560]{1,0:T(8,128)(2,1)}) %all-reduce.29.cloned.1.call-update) | async-done | bytes 327696 | tf_op jit(solution)/shard_map/psum | solution.py:39
  1084.5 37.1 %psum.223 = f32[64,64]{0,1:T(8,128)S(1)} all-reduce(f32[64,64]{0,1:T(8,128)S(1)} %fusion.127), channel_id=1, replica_groups=mesh['gene'=8,'cell'=4] {'gene'}, use_global_device_ids=true, to_apply=%region_43.47 | all-reduce | flops 4096 | bytes 32768 | tf_op jit(solution)/shard_map/psum | solution.py:42
  (167 shorter events, 184.6 us)
Async XLA Ops:
  6.5 222.6 %all-reduce.31.cloned.1.call-start = ((), (), s32[]{:S(2)}) async-start(), calls=%async_computation.7 | async-start | bytes 172032 | tf_op jit(solution)/shard_map/psum | solution.py:29
  175.0 11.6 %slice-start = ((s8[5242880]{0:T(1024)(128)(4,1)}), s8[1048576]{0:T(1024)(128)(4,1)S(1)}, s32[]{:S(2)}) async-start(s8[5242880]{0:T(1024)(128)(4,1)} %bitcast.200), calls=%async_computation.8 | async-start | bytes 2097152
  179.3 7.3 slice-start.1
  179.3 12.7 %slice-start.2 = ((s8[5242880]{0:T(1024)(128)(4,1)}), s8[4194304]{0:T(1024)(128)(4,1)S(1)}, s32[]{:S(2)}) async-start(s8[5242880]{0:T(1024)(128)(4,1)} %bitcast.202), calls=%async_computation.10 | async-start | bytes 8388608
  179.3 12.7 %slice-start.4 = ((s8[5242880]{0:T(1024)(128)(4,1)}), s8[4194304]{0:T(1024)(128)(4,1)S(1)}, s32[]{:S(2)}) async-start(s8[5242880]{0:T(1024)(128)(4,1)} %bitcast.204), calls=%async_computation.12 | async-start | bytes 8388608
  186.6 5.4 slice-start.3
  186.6 5.4 slice-start.5
  192.0 37.8 %copy-start = (f32[64,2560]{1,0:T(8,128)S(1)}, f32[64,2560]{1,0:T(8,128)}, u32[]{:S(2)}) copy-start(f32[64,2560]{1,0:T(8,128)} %param.10) | copy-start | bytes 1966084
  195.6 114.4 %all-reduce.17.cloned.1.call-start = ((), (), s32[]{:S(2)}) async-start(), calls=%async_computation | async-start | bytes 655360 | tf_op jit(solution)/shard_map/psum | solution.py:39
  234.5 45.4 %copy-start.6 = (f32[2560]{0:T(1024)S(1)}, f32[2560]{0:T(1024)}, u32[]{:S(2)}) copy-start(f32[2560]{0:T(1024)} %get-tuple-element.8) | copy-start | bytes 30724
  279.8 158.7 %all-reduce.19.cloned.1.call-start = ((), (), s32[]{:S(2)}) async-start(), calls=%async_computation.1 | async-start | bytes 655360 | tf_op jit(solution)/shard_map/psum | solution.py:39
  367.4 40.6 %copy-start.5 = (f32[2560]{0:T(1024)S(1)}, f32[2560]{0:T(1024)}, u32[]{:S(2)}) copy-start(f32[2560]{0:T(1024)} %get-tuple-element.10) | copy-start | bytes 30724
  408.0 159.9 %all-reduce.21.cloned.1.call-start = ((), (), s32[]{:S(2)}) async-start(), calls=%async_computation.2 | async-start | bytes 655360 | tf_op jit(solution)/shard_map/psum | solution.py:39
  496.6 40.6 %copy-start.4 = (f32[2560]{0:T(1024)S(1)}, f32[2560]{0:T(1024)}, u32[]{:S(2)}) copy-start(f32[2560]{0:T(1024)} %get-tuple-element.11) | copy-start | bytes 30724
  537.1 159.4 %all-reduce.23.cloned.1.call-start = ((), (), s32[]{:S(2)}) async-start(), calls=%async_computation.3 | async-start | bytes 655360 | tf_op jit(solution)/shard_map/psum | solution.py:39
  625.3 40.8 %copy-start.3 = (f32[2560]{0:T(1024)S(1)}, f32[2560]{0:T(1024)}, u32[]{:S(2)}) copy-start(f32[2560]{0:T(1024)} %get-tuple-element.12) | copy-start | bytes 30724
  665.9 159.4 %all-reduce.25.cloned.1.call-start = ((), (), s32[]{:S(2)}) async-start(), calls=%async_computation.4 | async-start | bytes 655360 | tf_op jit(solution)/shard_map/psum | solution.py:39
  754.0 40.6 %copy-start.2 = (f32[2560]{0:T(1024)S(1)}, f32[2560]{0:T(1024)}, u32[]{:S(2)}) copy-start(f32[2560]{0:T(1024)} %get-tuple-element.13) | copy-start | bytes 30724
  794.5 159.6 %all-reduce.27.cloned.1.call-start = ((), (), s32[]{:S(2)}) async-start(), calls=%async_computation.5 | async-start | bytes 655360 | tf_op jit(solution)/shard_map/psum | solution.py:39
  882.8 40.9 %copy-start.1 = (f32[2560]{0:T(1024)S(1)}, f32[2560]{0:T(1024)}, u32[]{:S(2)}) copy-start(f32[2560]{0:T(1024)} %get-tuple-element.14) | copy-start | bytes 30724
  923.5 159.2 %all-reduce.29.cloned.1.call-start = ((), (), s32[]{:S(2)}) async-start(), calls=%async_computation.6 | async-start | bytes 655360 | tf_op jit(solution)/shard_map/psum | solution.py:39
Sparse Core Ops, SparseCore 0:
  195.7 33.3 all-reduce.30
  280.0 29.9 all-reduce.16
  408.1 30.4 all-reduce.18
  537.3 30.5 all-reduce.20
  666.0 30.5 all-reduce.22
  794.7 30.5 all-reduce.24
  923.7 30.4 all-reduce.26
  1052.2 30.4 all-reduce.28
where the time goes:
time: 1150 us; the launch traced here: 1140 us
  blocking collectives  517 us (45%)
  waiting for transfers between devices  247 us (21%)
  local copies, waits for them, and re-layouts  168 us (15%)
  other arithmetic  108 us (9%)
  matrix products  88.8 us (8%)
  between operations  14.4 us (1%)
    psum x7, blocking collectives, shards(): gram_matrix = lax.psum(gram_part, 'gene')  260 us
    psum x7, blocking collectives, shards(): scores = lax.psum(partial_value, 'gene')  257 us
    psum x7, waiting for transfers between devices, shards(): lax.psum(local_update.astype(jnp.bfloat16), 'cell').astype(jnp.float32)  213 us
    gather x7, local copies, waits for them, and re-layouts, shards(): gathered = jnp.take(pool_counts, chosen, axis=1)  141 us
    another operation x21, other arithmetic, shards(): factor = jnp.linalg.cholesky(gram_matrix)  45.6 us
    another operation x14, other arithmetic, shards(): lax.linalg.triangular_solve(factor, stepped, left_side=True, lower=True)  38.8 us
    psum x1, waiting for transfers between devices, shards(): batch_means = lax.psum(local_sums, 'cell') / batch_total  33.5 us
    dot_general x7, matrix products, transposed_product(): lax.dot_general(left, right, (((1,), (1,)), ((), ())), preferred_element_...  30.7 us
  transfers between devices with their start and end apart: 8, of which 8 were waited for; matrix products, arithmetic and copies ran while one was open for 0% of the time, Pallas kernels for 0%

commit v1 on v0

--- a/solution.py
+++ b/solution.py
@@ -36,7 +36,9 @@
         raw_update = transposed_product(scores_low, gathered)
         row_totals = jnp.sum(scores_low, axis=1, dtype=jnp.float32)
         local_update = (raw_update - row_totals[:, None] * batch_means[None, :]) / batch_total
-        update = lax.psum(local_update.astype(jnp.bfloat16), "cell").astype(jnp.float32)
+        update = jnp.sum(lax.all_gather(local_update.astype(jnp.bfloat16), "cell"), axis=0).astype(
+            jnp.float32
+        )
         stepped = loadings + step_rate * update
         gram_part = jnp.dot(stepped, stepped.T, precision=lax.Precision.HIGHEST)
         gram_matrix = lax.psum(gram_part, "gene")

time: 1150 us -> 1050 us (0.913)
  waiting for transfers between devices: 247 us -> 149 us
  matrix products: 88.8 us -> 74 us
    psum x7 -> x0, waiting for transfers between devices: 213 us -> none  [shards(): lax.psum(local_update.astype(jnp.bfloat16), 'cell').astype(jnp.float32)]
    all_gather x0 -> x7, waiting for transfers between devices: none -> 116 us  [shards(): lax.all_gather(local_update.astype(jnp.bfloat16), 'cell')]
where the time goes in v1:
time: 1050 us; the launch traced here: 1040 us
  blocking collectives  518 us (49%)
  local copies, waits for them, and re-layouts  168 us (16%)
  waiting for transfers between devices  149 us (14%)
  other arithmetic  118 us (11%)
  matrix products  74 us (7%)
  between operations  14.4 us (1%)
    psum x7, blocking collectives, shards(): gram_matrix = lax.psum(gram_part, 'gene')  260 us
    psum x7, blocking collectives, shards(): scores = lax.psum(partial_value, 'gene')  257 us
    gather x7, local copies, waits for them, and re-layouts, shards(): gathered = jnp.take(pool_counts, chosen, axis=1)  141 us
    all_gather x7, waiting for transfers between devices, shards(): lax.all_gather(local_update.astype(jnp.bfloat16), 'cell')  116 us
    another operation x21, other arithmetic, shards(): factor = jnp.linalg.cholesky(gram_matrix)  45.6 us
    another operation x14, other arithmetic, shards(): lax.linalg.triangular_solve(factor, stepped, left_side=True, lower=True)  38.8 us
    psum x1, waiting for transfers between devices, shards(): batch_means = lax.psum(local_sums, 'cell') / batch_total  33.5 us
    dot_general x7, matrix products, transposed_product(): lax.dot_general(left, right, (((1,), (1,)), ((), ())), preferred_element_...  30.8 us
  transfers between devices with their start and end apart: 8, of which 8 were waited for; matrix products, arithmetic and copies ran while one was open for 0% of the time, Pallas kernels for 0%

profile of v1, /device:TPU:0, one launch (start us, length us, event | category | flops | bytes accessed | tf_op | source)
XLA Modules:
  0.0 1042.1 jit_solution(1881611622029403148)
XLA Ops:
  7.8 25.9 %copy.4 = bf16[2560,4096]{0,1:T(8,128)(2,1)} copy(bf16[2560,4096]{1,0:T(8,128)(2,1)} %param.8) | data formatting | bytes 41943040 | tf_op args[0]
  33.7 20.2 %gather_fusion.6 = bf16[1024,2560]{1,0:T(8,128)(2,1)} fusion(bf16[2560,4096]{0,1:T(8,128)(2,1)} %copy.4, s32[1024]{0:T(1024)S(1)} %fusion.188), kind=kCustom, calls=%fused_computation.6.clone | custom fusion | bytes 10489856 | tf_op jit(solution)/shard_map/jit(_take)/gather | solution.py:25
  53.8 20.1 %gather_fusion.5 = bf16[1024,2560]{1,0:T(8,128)(2,1)} fusion(bf16[2560,4096]{0,1:T(8,128)(2,1)} %copy.4, s32[1024]{0:T(1024)S(1)} %fusion.187), kind=kCustom, calls=%fused_computation.5.clone | custom fusion | bytes 10489856 | tf_op jit(solution)/shard_map/jit(_take)/gather | solution.py:25
  73.9 20.5 %gather_fusion.4 = bf16[1024,2560]{1,0:T(8,128)(2,1)} fusion(bf16[2560,4096]{0,1:T(8,128)(2,1)} %copy.4, s32[1024]{0:T(1024)S(1)} %fusion.186), kind=kCustom, calls=%fused_computation.4.clone | custom fusion | bytes 10489856 | tf_op jit(solution)/shard_map/jit(_take)/gather | solution.py:25
  94.5 20.1 %gather_fusion.3 = bf16[1024,2560]{1,0:T(8,128)(2,1)} fusion(bf16[2560,4096]{0,1:T(8,128)(2,1)} %copy.4, s32[1024]{0:T(1024)S(1)} %fusion.185), kind=kCustom, calls=%fused_computation.3.clone | custom fusion | bytes 10489856 | tf_op jit(solution)/shard_map/jit(_take)/gather | solution.py:25
  114.6 20.2 %gather_fusion.2 = bf16[1024,2560]{1,0:T(8,128)(2,1)} fusion(bf16[2560,4096]{0,1:T(8,128)(2,1)} %copy.4, s32[1024]{0:T(1024)S(1)} %fusion.184), kind=kCustom, calls=%fused_computation.2.clone | custom fusion | bytes 10489856 | tf_op jit(solution)/shard_map/jit(_take)/gather | solution.py:25
  134.8 20.1 %gather_fusion.1 = bf16[1024,2560]{1,0:T(8,128)(2,1)} fusion(bf16[2560,4096]{0,1:T(8,128)(2,1)} %copy.4, s32[1024]{0:T(1024)S(1)} %fusion.183), kind=kCustom, calls=%fused_computation.1.clone | custom fusion | bytes 10489856 | tf_op jit(solution)/shard_map/jit(_take)/gather | solution.py:25
  154.9 20.1 %gather_fusion = bf16[1024,2560]{1,0:T(8,128)(2,1)} fusion(bf16[2560,4096]{0,1:T(8,128)(2,1)} %copy.4, s32[1024]{0:T(1024)S(1)} %fusion.182), kind=kCustom, calls=%fused_computation.clone | custom fusion | bytes 10489856 | tf_op jit(solution)/shard_map/jit(_take)/gather | solution.py:25
  179.3 7.3 convert_reduce_fusion
  195.6 33.5 %all-reduce.10.cloned.1.call-done = (f32[2560]{0:T(1024)}, f32[2560]{0:T(1024)}, f32[2560]{0:T(1024)}, f32[2560]{0:T(1024)}, f32[2560]{0:T(1024)}, /*index=5*/f32[2560]{0:T(1024)}, f32[2560]{0:T(1024)}) async-done(((f32[2560]{0:T(1024)}, f32[2560]{0:T(1024)}, f32[2560]{0:T(1024)}, f32[2560]{0:T(1024)}, f32[2560]{0:T(1024)}, /*index=5*/f32[2560]{0:T(1024)}, f32[2560]{0:T(1024)}), (f32[2560]{0:T(1024)}, ...) | async-done | bytes 71696 | tf_op jit(solution)/shard_map/psum | solution.py:29
  234.5 40.8 %all-reduce.11 = bf16[64,1024]{1,0:T(8,128)(2,1)S(1)} all-reduce(f32[64,1024]{1,0:T(8,128)S(1)} %fusion.94), channel_id=1, replica_groups=mesh['gene'=8,'cell'=4] {'gene'}, use_global_device_ids=true, to_apply=%region_2.4 | all-reduce | flops 65536 | bytes 393216 | tf_op jit(solution)/shard_map/psum | solution.py:34
  279.9 15.6 %all-gather.15.cloned.1.call-done = bf16[256,2560]{1,0:T(8,128)(2,1)} async-done(((bf16[64,2560]{1,0:T(8,128)(2,1)}), bf16[256,2560]{1,0:T(8,128)(2,1)}) %all-gather.15.cloned.1.call-update) | async-done | bytes 1310736 | tf_op jit(solution)/shard_map/all_gather | solution.py:39
  297.8 37.1 %psum.149 = f32[64,64]{0,1:T(8,128)S(1)} all-reduce(f32[64,64]{0,1:T(8,128)S(1)} %fusion.116), channel_id=1, replica_groups=mesh['gene'=8,'cell'=4] {'gene'}, use_global_device_ids=true, to_apply=%region_5.7 | all-reduce | flops 4096 | bytes 32768 | tf_op jit(solution)/shard_map/psum | solution.py:44
  352.5 35.9 %all-reduce.12 = bf16[64,1024]{1,0:T(8,128)(2,1)S(1)} all-reduce(f32[64,1024]{1,0:T(8,128)S(1)} %fusion.97), channel_id=1, replica_groups=mesh['gene'=8,'cell'=4] {'gene'}, use_global_device_ids=true, to_apply=%region_10.0 | all-reduce | flops 65536 | bytes 393216 | tf_op jit(solution)/shard_map/psum | solution.py:34
  393.0 16.8 %all-gather.17.cloned.1.call-done = bf16[256,2560]{1,0:T(8,128)(2,1)} async-done(((bf16[64,2560]{1,0:T(8,128)(2,1)}), bf16[256,2560]{1,0:T(8,128)(2,1)}) %all-gather.17.cloned.1.call-update) | async-done | bytes 1310736 | tf_op jit(solution)/shard_map/all_gather | solution.py:39
  412.0 37.6 %psum.152 = f32[64,64]{0,1:T(8,128)S(1)} all-reduce(f32[64,64]{0,1:T(8,128)S(1)} %fusion.118), channel_id=1, replica_groups=mesh['gene'=8,'cell'=4] {'gene'}, use_global_device_ids=true, to_apply=%region_13.0 | all-reduce | flops 4096 | bytes 32768 | tf_op jit(solution)/shard_map/psum | solution.py:44
  467.3 36.1 %all-reduce.13 = bf16[64,1024]{1,0:T(8,128)(2,1)S(1)} all-reduce(f32[64,1024]{1,0:T(8,128)S(1)} %fusion.100), channel_id=1, replica_groups=mesh['gene'=8,'cell'=4] {'gene'}, use_global_device_ids=true, to_apply=%region_16.0 | all-reduce | flops 65536 | bytes 393216 | tf_op jit(solution)/shard_map/psum | solution.py:34
  508.0 16.4 %all-gather.19.cloned.1.call-done = bf16[256,2560]{1,0:T(8,128)(2,1)} async-done(((bf16[64,2560]{1,0:T(8,128)(2,1)}), bf16[256,2560]{1,0:T(8,128)(2,1)}) %all-gather.19.cloned.1.call-update) | async-done | bytes 1310736 | tf_op jit(solution)/shard_map/all_gather | solution.py:39
  526.6 37.1 %psum.155 = f32[64,64]{0,1:T(8,128)S(1)} all-reduce(f32[64,64]{0,1:T(8,128)S(1)} %fusion.120), channel_id=1, replica_groups=mesh['gene'=8,'cell'=4] {'gene'}, use_global_device_ids=true, to_apply=%region_19.0 | all-reduce | flops 4096 | bytes 32768 | tf_op jit(solution)/shard_map/psum | solution.py:44
  581.3 35.9 %all-reduce.14 = bf16[64,1024]{1,0:T(8,128)(2,1)S(1)} all-reduce(f32[64,1024]{1,0:T(8,128)S(1)} %fusion.103), channel_id=1, replica_groups=mesh['gene'=8,'cell'=4] {'gene'}, use_global_device_ids=true, to_apply=%region_22.0 | all-reduce | flops 65536 | bytes 393216 | tf_op jit(solution)/shard_map/psum | solution.py:34
  622.0 16.7 %all-gather.21.cloned.1.call-done = bf16[256,2560]{1,0:T(8,128)(2,1)} async-done(((bf16[64,2560]{1,0:T(8,128)(2,1)}), bf16[256,2560]{1,0:T(8,128)(2,1)}) %all-gather.21.cloned.1.call-update) | async-done | bytes 1310736 | tf_op jit(solution)/shard_map/all_gather | solution.py:39
  640.9 37.1 %psum.158 = f32[64,64]{0,1:T(8,128)S(1)} all-reduce(f32[64,64]{0,1:T(8,128)S(1)} %fusion.122), channel_id=1, replica_groups=mesh['gene'=8,'cell'=4] {'gene'}, use_global_device_ids=true, to_apply=%region_25.0 | all-reduce | flops 4096 | bytes 32768 | tf_op jit(solution)/shard_map/psum | solution.py:44
  678.1 5.8 cholesky.152
  695.6 36.1 %all-reduce.15 = bf16[64,1024]{1,0:T(8,128)(2,1)S(1)} all-reduce(f32[64,1024]{1,0:T(8,128)S(1)} %fusion.106), channel_id=1, replica_groups=mesh['gene'=8,'cell'=4] {'gene'}, use_global_device_ids=true, to_apply=%region_28.0 | all-reduce | flops 65536 | bytes 393216 | tf_op jit(solution)/shard_map/psum | solution.py:34
  736.3 16.9 %all-gather.23.cloned.1.call-done = bf16[256,2560]{1,0:T(8,128)(2,1)} async-done(((bf16[64,2560]{1,0:T(8,128)(2,1)}), bf16[256,2560]{1,0:T(8,128)(2,1)}) %all-gather.23.cloned.1.call-update) | async-done | bytes 1310736 | tf_op jit(solution)/shard_map/all_gather | solution.py:39
  755.5 37.1 %psum.161 = f32[64,64]{0,1:T(8,128)S(1)} all-reduce(f32[64,64]{0,1:T(8,128)S(1)} %fusion.124), channel_id=1, replica_groups=mesh['gene'=8,'cell'=4] {'gene'}, use_global_device_ids=true, to_apply=%region_31.0 | all-reduce | flops 4096 | bytes 32768 | tf_op jit(solution)/shard_map/psum | solution.py:44
  810.2 36.3 %all-reduce.16 = bf16[64,1024]{1,0:T(8,128)(2,1)S(1)} all-reduce(f32[64,1024]{1,0:T(8,128)S(1)} %fusion.109), channel_id=1, replica_groups=mesh['gene'=8,'cell'=4] {'gene'}, use_global_device_ids=true, to_apply=%region_34.0 | all-reduce | flops 65536 | bytes 393216 | tf_op jit(solution)/shard_map/psum | solution.py:34
  851.1 16.9 %all-gather.25.cloned.1.call-done = bf16[256,2560]{1,0:T(8,128)(2,1)} async-done(((bf16[64,2560]{1,0:T(8,128)(2,1)}), bf16[256,2560]{1,0:T(8,128)(2,1)}) %all-gather.25.cloned.1.call-update) | async-done | bytes 1310736 | tf_op jit(solution)/shard_map/all_gather | solution.py:39
  870.3 37.1 %psum.164 = f32[64,64]{0,1:T(8,128)S(1)} all-reduce(f32[64,64]{0,1:T(8,128)S(1)} %fusion.126), channel_id=1, replica_groups=mesh['gene'=8,'cell'=4] {'gene'}, use_global_device_ids=true, to_apply=%region_37.0 | all-reduce | flops 4096 | bytes 32768 | tf_op jit(solution)/shard_map/psum | solution.py:44
  925.0 36.0 %all-reduce.17 = bf16[64,1024]{1,0:T(8,128)(2,1)S(1)} all-reduce(f32[64,1024]{1,0:T(8,128)S(1)} %fusion.112), channel_id=1, replica_groups=mesh['gene'=8,'cell'=4] {'gene'}, use_global_device_ids=true, to_apply=%region_40.0 | all-reduce | flops 65536 | bytes 393216 | tf_op jit(solution)/shard_map/psum | solution.py:34
  965.5 16.5 %all-gather.27.cloned.1.call-done = bf16[256,2560]{1,0:T(8,128)(2,1)} async-done(((bf16[64,2560]{1,0:T(8,128)(2,1)}), bf16[256,2560]{1,0:T(8,128)(2,1)}) %all-gather.27.cloned.1.call-update) | async-done | bytes 1310736 | tf_op jit(solution)/shard_map/all_gather | solution.py:39
  984.2 37.1 %psum.167 = f32[64,64]{0,1:T(8,128)S(1)} all-reduce(f32[64,64]{0,1:T(8,128)S(1)} %fusion.127), channel_id=1, replica_groups=mesh['gene'=8,'cell'=4] {'gene'}, use_global_device_ids=true, to_apply=%region_43.47 | all-reduce | flops 4096 | bytes 32768 | tf_op jit(solution)/shard_map/psum | solution.py:44
  (174 shorter events, 180.6 us)
Async XLA Ops:
  6.5 222.6 %all-reduce.10.cloned.1.call-start = ((), (), s32[]{:S(2)}) async-start(), calls=%async_computation.7 | async-start | bytes 172032 | tf_op jit(solution)/shard_map/psum | solution.py:29
  175.0 11.6 %slice-start = ((s8[5242880]{0:T(1024)(128)(4,1)}), s8[1048576]{0:T(1024)(128)(4,1)S(1)}, s32[]{:S(2)}) async-start(s8[5242880]{0:T(1024)(128)(4,1)} %bitcast.207), calls=%async_computation.8 | async-start | bytes 2097152
  179.3 7.3 slice-start.1
  179.3 12.7 %slice-start.2 = ((s8[5242880]{0:T(1024)(128)(4,1)}), s8[4194304]{0:T(1024)(128)(4,1)S(1)}, s32[]{:S(2)}) async-start(s8[5242880]{0:T(1024)(128)(4,1)} %bitcast.209), calls=%async_computation.10 | async-start | bytes 8388608
  179.3 12.7 %slice-start.4 = ((s8[5242880]{0:T(1024)(128)(4,1)}), s8[4194304]{0:T(1024)(128)(4,1)S(1)}, s32[]{:S(2)}) async-start(s8[5242880]{0:T(1024)(128)(4,1)} %bitcast.211), calls=%async_computation.12 | async-start | bytes 8388608
  186.6 5.4 slice-start.3
  186.6 5.4 slice-start.5
  192.0 37.8 %copy-start = (f32[64,2560]{1,0:T(8,128)S(1)}, f32[64,2560]{1,0:T(8,128)}, u32[]{:S(2)}) copy-start(f32[64,2560]{1,0:T(8,128)} %param.10) | copy-start | bytes 1966084
  195.6 100.0 %all-gather.15.cloned.1.call-start = ((), (), s32[]{:S(2)}) async-start(), calls=%async_computation | async-start | bytes 1638400 | tf_op jit(solution)/shard_map/all_gather | solution.py:39
  234.5 45.4 %copy-start.6 = (f32[2560]{0:T(1024)S(1)}, f32[2560]{0:T(1024)}, u32[]{:S(2)}) copy-start(f32[2560]{0:T(1024)} %get-tuple-element.8) | copy-start | bytes 30724
  279.8 130.0 %all-gather.17.cloned.1.call-start = ((), (), s32[]{:S(2)}) async-start(), calls=%async_computation.1 | async-start | bytes 1638400 | tf_op jit(solution)/shard_map/all_gather | solution.py:39
  352.5 40.5 %copy-start.5 = (f32[2560]{0:T(1024)S(1)}, f32[2560]{0:T(1024)}, u32[]{:S(2)}) copy-start(f32[2560]{0:T(1024)} %get-tuple-element.10) | copy-start | bytes 30724
  393.0 131.4 %all-gather.19.cloned.1.call-start = ((), (), s32[]{:S(2)}) async-start(), calls=%async_computation.2 | async-start | bytes 1638400 | tf_op jit(solution)/shard_map/all_gather | solution.py:39
  467.3 40.7 %copy-start.4 = (f32[2560]{0:T(1024)S(1)}, f32[2560]{0:T(1024)}, u32[]{:S(2)}) copy-start(f32[2560]{0:T(1024)} %get-tuple-element.11) | copy-start | bytes 30724
  508.0 130.7 %all-gather.21.cloned.1.call-start = ((), (), s32[]{:S(2)}) async-start(), calls=%async_computation.3 | async-start | bytes 1638400 | tf_op jit(solution)/shard_map/all_gather | solution.py:39
  581.3 40.6 %copy-start.3 = (f32[2560]{0:T(1024)S(1)}, f32[2560]{0:T(1024)}, u32[]{:S(2)}) copy-start(f32[2560]{0:T(1024)} %get-tuple-element.12) | copy-start | bytes 30724
  621.7 131.5 %all-gather.23.cloned.1.call-start = ((), (), s32[]{:S(2)}) async-start(), calls=%async_computation.4 | async-start | bytes 1638400 | tf_op jit(solution)/shard_map/all_gather | solution.py:39
  695.6 40.7 %copy-start.2 = (f32[2560]{0:T(1024)S(1)}, f32[2560]{0:T(1024)}, u32[]{:S(2)}) copy-start(f32[2560]{0:T(1024)} %get-tuple-element.13) | copy-start | bytes 30724
  736.2 131.8 %all-gather.25.cloned.1.call-start = ((), (), s32[]{:S(2)}) async-start(), calls=%async_computation.5 | async-start | bytes 1638400 | tf_op jit(solution)/shard_map/all_gather | solution.py:39
  810.2 40.9 %copy-start.1 = (f32[2560]{0:T(1024)S(1)}, f32[2560]{0:T(1024)}, u32[]{:S(2)}) copy-start(f32[2560]{0:T(1024)} %get-tuple-element.14) | copy-start | bytes 30724
  851.0 130.9 %all-gather.27.cloned.1.call-start = ((), (), s32[]{:S(2)}) async-start(), calls=%async_computation.6 | async-start | bytes 1638400 | tf_op jit(solution)/shard_map/all_gather | solution.py:39
Sparse Core Ops, SparseCore 0:
  195.7 33.3 all-reduce.9
  280.0 15.5 all-gather.14
  393.1 16.6 all-gather.16
  508.1 16.2 all-gather.18
  621.9 16.7 all-gather.20
  736.4 16.8 all-gather.22
  851.1 16.8 all-gather.24
  965.6 16.2 all-gather.26
